TPU v7x, 128 devices: a whole 4x4x4 slice. The times are simulated.
128 devices in a mesh: row: 8 (over z, core), col: 16 (over y, x).
Axes of the slice: x: 4, y: 4, z: 4, core: 2. Of those that a mesh axis runs over, the one named last changes fastest.
Arguments:
- grad_out: bfloat16 [131072, 256], P(('row', 'col')), may hold values from -6 to 6
- rel_weight: bfloat16 [4, 256, 256], replicated, may hold values from -0.375 to 0.375
- adjacency: bfloat16 [24576, 128, 128], P(('row', 'col')), may hold values from -0.5 to 0.5
- block_row: int32 [24576], P(('row', 'col')), may hold values from 0 to 127, as said below
- block_col: int32 [24576], P(('row', 'col')), may hold values from 0 to 63
- type_count: int32 [512], P(('row', 'col')), may hold values from 0 to 192, as said below
Outputs:
- grad_in: float32 [131072, 256], P(('row', 'col'))
Inputs may be any that keep to these rules, and one draw needn't show every extreme that they name: `block_row`: among all 192 slots of one tile, at most 4 distinct values fall in any aligned range of 8 values (the node blocks of one device of the tile row), and in every tile some range holds exactly 4. `type_count`: A tile's 4 counts sum to at most 192; in some tile a single type holds all 192 slots.
All inputs are finite; a program needn't handle non-finite values.
Results may differ from a plain program's by a relative error of at most 0.012.
Values may be sent and summed in bfloat16 or wider, within the bound.
A program may use at most 192 MiB of HBM per device.

v0:
```python
import math
import jax
import jax.numpy as jnp
from jax import lax
from jax.sharding import PartitionSpec as P


def per_device(grad_out, rel_weight, adjacency, block_row, block_col, type_count):
    ncols = lax.axis_size("col")
    nrows = lax.axis_size("row")
    blk = adjacency.shape[1]
    feat = grad_out.shape[1]
    kinds = rel_weight.shape[0]
    owned = grad_out.shape[0] // blk
    slots_total = adjacency.shape[0]
    wcat = jnp.transpose(rel_weight, (2, 0, 1)).reshape(feat, kinds * feat)
    gathered = jnp.dot(
        lax.all_gather(grad_out, "col", axis=0, tiled=True),
        wcat,
        preferred_element_type=jnp.float32,
    ).astype(jnp.bfloat16)
    table = gathered.reshape(ncols * owned, blk, kinds, feat)
    ends = jnp.cumsum(type_count)
    total = ends[kinds - 1]
    position = jnp.arange(slots_total, dtype=jnp.int32)
    kind = jnp.minimum(
        jnp.sum((position[:, None] >= ends[None, :]).astype(jnp.int32), axis=1), kinds - 1
    )
    live = position < total
    group = math.gcd(slots_total, 64)
    groups = slots_total // group
    partial_start = jnp.zeros((nrows * owned, blk, feat), jnp.float32)

    def step(index, partial_value):
        start = index * group
        adj_part = lax.dynamic_slice_in_dim(adjacency, start, group, 0)
        slot_part = lax.dynamic_slice_in_dim(block_row, start, group, 0)
        kind_part = lax.dynamic_slice_in_dim(kind, start, group, 0)
        live_part = lax.dynamic_slice_in_dim(live, start, group, 0)
        col_part = lax.dynamic_slice_in_dim(block_col, start, group, 0)
        picked = table[slot_part, :, kind_part, :]
        term = jnp.einsum("kab,kaf->kbf", adj_part, picked, preferred_element_type=jnp.float32)
        term = jnp.where(live_part[:, None, None], term, jnp.float32(0.0))
        return partial_value.at[col_part].add(term)

    partial_value = lax.fori_loop(0, groups, step, partial_start)
    return lax.psum_scatter(
        partial_value.reshape(nrows * owned * blk, feat).astype(jnp.bfloat16),
        "row",
        scatter_dimension=0,
        tiled=True,
    ).astype(jnp.float32)


def solution(mesh):
    in_specs = (
        P(("row", "col"), None),
        P(),
        P(("row", "col"), None, None),
        P(("row", "col")),
        P(("row", "col")),
        P(("row", "col")),
    )
    out_specs = P(("row", "col"), None)
    return jax.shard_map(
        per_device, mesh=mesh, in_specs=in_specs, out_specs=out_specs, check_vma=False
    )
```

profile of v0, /device:TPU:0, one launch (start us, length us, event | category | flops | bytes accessed | tf_op | source)
XLA Modules:
  0.0 332.7 jit_solution(6268306720380920505)
XLA Ops:
  6.5 0.0 copy-start
  6.5 0.0 all-gather.2.cloned.1.call-start
  6.5 0.7 all-gather.2.cloned.1.call-update
  7.3 0.0 reduce-scatter.2.cloned.1.call-start
  7.3 0.8 reduce-window.4
  8.1 0.6 slice.4
  8.7 0.6 iota_compare_fusion.1
  9.3 0.1 convert_reduce_fusion
  9.4 73.3 %all-gather.2.cloned.1.call-done = bf16[16384,256]{1,0:T(8,128)(2,1)} async-done(((bf16[1024,256]{1,0:T(8,128)(2,1)}), bf16[16384,256]{1,0:T(8,128)(2,1)}) %all-gather.2.cloned.1.call-update) | async-done | bytes 8388624 | tf_op jit(solution)/shard_map/all_gather | solution.py:18
  82.7 0.0 copy-done
  82.7 17.5 %convolution_convert_fusion = bf16[16384,1024]{1,0:T(8,128)(2,1)} fusion(bf16[16384,256]{1,0:T(8,128)(2,1)} %all-gather.2.cloned.1.call-done, bf16[256,1024]{0,1:T(8,128)(2,1)S(1)} %bitcast.12), kind=kOutput, calls=%fused_computation.13 | convolution fusion | flops 8606711808 | bytes 42467328 | tf_op jit(solution)/shard_map/dot_general | solution.py:17
  100.1 54.7 %reshape.19 = bf16[128,128,4,256]{3,2,1,0:T(4,128)(2,1)} reshape(bf16[16384,1024]{1,0:T(8,128)(2,1)} %convolution_convert_fusion) | data formatting | bytes 67108864 | tf_op jit(solution)/shard_map/reshape | solution.py:22
  154.8 23.0 %copy.12 = bf16[128,128,4,256]{3,1,2,0:T(8,128)(2,1)} copy(bf16[128,128,4,256]{3,2,1,0:T(4,128)(2,1)} %reshape.19) | data formatting | bytes 67108864 | tf_op jit(solution)/shard_map/while | solution.py:46
  177.9 0.0 copy-start.2
  177.9 0.0 copy-start.3
  177.9 4.2 %broadcast_in_dim.53 = f32[64,128,256]{2,1,0:T(8,128)} broadcast(f32[]{:T(128)} %constant.55.clone.1), dimensions={} | broadcast | bytes 8388612 | tf_op jit(solution)/shard_map/broadcast_in_dim | solution.py:32
  182.1 0.0 copy-done.2
  182.1 0.0 copy-done.3
  182.1 97.6 %while.13 = (s32[]{:T(128)}, f32[64,128,256]{2,1,0:T(8,128)}, s32[192]{0:T(256)S(1)}, pred[192]{0:T(512)(128)(4,1)S(1)}, bf16[192,128,128]{2,1,0:T(8,128)(2,1)},...) while((s32[]{:T(128)}, f32[64,128,256]{2,1,0:T(8,128)}, ...), condition=%wide.region_4.5_spmd, body=%wide.region_2.4_spmd.sunk | while | flops 541066112 | bytes 48236912 | solution.py:46
  182.1 0.1 compare_select_fusion.4
  182.2 5.2 %gather_fusion = bf16[64,128,256]{2,1,0:T(8,128)(2,1)} fusion(bf16[128,128,4,256]{3,1,2,0:T(8,128)(2,1)} %get-tuple-element.271, s32[64]{0:T(128)S(1)} %get-tuple-element.239), kind=kCustom, calls=%fused_computation.clone.1 | custom fusion | bytes 8389120 | tf_op jit(solution)/shard_map/while/body/eval_jaxpr/gather | solution.py:41
  187.3 0.1 dynamic_slice.45
  187.4 7.6 %broadcast_select_fusion.2 = f32[64,128,256]{2,1,0:T(8,128)} fusion(pred[64]{0:T(512)(128)(4,1)S(1)} %dynamic_slice.45, bf16[64,128,256]{2,1,0:T(8,128)(2,1)} %gather_fusion, bf16[192,128,128]{2,1,0:T(8,128)(2,1)} %get-tuple-element.268, s32[]{:T(128)S(6)} %select_n.61), kind=kOutput, calls=%fused_computation.2.clone.1 | convolution fusion | flops 538968064 | bytes 14680132 | tf_op jit(solution)/shard_map/while/body/eval_jaxpr/kab,kaf->kbf/dot_general | solution.py:42
  195.0 19.6 %scatter_fusion = f32[64,128,256]{2,1,0:T(8,128)} fusion(f32[64,128,256]{2,1,0:T(8,128)} %get-tuple-element.253, s32[64]{0:T(128)S(1)} %get-tuple-element.238, f32[64,128,256]{2,1,0:T(8,128)} %broadcast_select_fusion.2), kind=kCustom, calls=%fused_computation.1.clone.1 | custom fusion | flops 2097152 | bytes 25166080 | tf_op jit(solution)/shard_map/while/body/eval_jaxpr/scatter-add | solution.py:44
  214.6 0.1 compare_select_fusion.4
  214.7 5.4 %gather_fusion = bf16[64,128,256]{2,1,0:T(8,128)(2,1)} fusion(bf16[128,128,4,256]{3,1,2,0:T(8,128)(2,1)} %get-tuple-element.271, s32[64]{0:T(128)S(1)} %get-tuple-element.239), kind=kCustom, calls=%fused_computation.clone.1 | custom fusion | bytes 8389120 | tf_op jit(solution)/shard_map/while/body/eval_jaxpr/gather | solution.py:41
  220.1 0.1 dynamic_slice.45
  220.2 7.6 %broadcast_select_fusion.2 = f32[64,128,256]{2,1,0:T(8,128)} fusion(pred[64]{0:T(512)(128)(4,1)S(1)} %dynamic_slice.45, bf16[64,128,256]{2,1,0:T(8,128)(2,1)} %gather_fusion, bf16[192,128,128]{2,1,0:T(8,128)(2,1)} %get-tuple-element.268, s32[]{:T(128)S(6)} %select_n.61), kind=kOutput, calls=%fused_computation.2.clone.1 | convolution fusion | flops 538968064 | bytes 14680132 | tf_op jit(solution)/shard_map/while/body/eval_jaxpr/kab,kaf->kbf/dot_general | solution.py:42
  227.8 19.6 %scatter_fusion = f32[64,128,256]{2,1,0:T(8,128)} fusion(f32[64,128,256]{2,1,0:T(8,128)} %get-tuple-element.253, s32[64]{0:T(128)S(1)} %get-tuple-element.238, f32[64,128,256]{2,1,0:T(8,128)} %broadcast_select_fusion.2), kind=kCustom, calls=%fused_computation.1.clone.1 | custom fusion | flops 2097152 | bytes 25166080 | tf_op jit(solution)/shard_map/while/body/eval_jaxpr/scatter-add | solution.py:44
  247.3 0.1 compare_select_fusion.4
  247.4 5.3 %gather_fusion = bf16[64,128,256]{2,1,0:T(8,128)(2,1)} fusion(bf16[128,128,4,256]{3,1,2,0:T(8,128)(2,1)} %get-tuple-element.271, s32[64]{0:T(128)S(1)} %get-tuple-element.239), kind=kCustom, calls=%fused_computation.clone.1 | custom fusion | bytes 8389120 | tf_op jit(solution)/shard_map/while/body/eval_jaxpr/gather | solution.py:41
  252.7 0.1 dynamic_slice.45
  252.8 7.6 %broadcast_select_fusion.2 = f32[64,128,256]{2,1,0:T(8,128)} fusion(pred[64]{0:T(512)(128)(4,1)S(1)} %dynamic_slice.45, bf16[64,128,256]{2,1,0:T(8,128)(2,1)} %gather_fusion, bf16[192,128,128]{2,1,0:T(8,128)(2,1)} %get-tuple-element.268, s32[]{:T(128)S(6)} %select_n.61), kind=kOutput, calls=%fused_computation.2.clone.1 | convolution fusion | flops 538968064 | bytes 14680132 | tf_op jit(solution)/shard_map/while/body/eval_jaxpr/kab,kaf->kbf/dot_general | solution.py:42
  260.3 19.4 %scatter_fusion = f32[64,128,256]{2,1,0:T(8,128)} fusion(f32[64,128,256]{2,1,0:T(8,128)} %get-tuple-element.253, s32[64]{0:T(128)S(1)} %get-tuple-element.238, f32[64,128,256]{2,1,0:T(8,128)} %broadcast_select_fusion.2), kind=kCustom, calls=%fused_computation.1.clone.1 | custom fusion | flops 2097152 | bytes 25166080 | tf_op jit(solution)/shard_map/while/body/eval_jaxpr/scatter-add | solution.py:44
  279.7 0.0 copy-start.1
  279.7 6.0 %convert_element_type.17 = bf16[64,128,256]{2,1,0:T(8,128)(2,1)} convert(f32[64,128,256]{2,1,0:T(8,128)} %get-tuple-element.144) | non-fusion elementwise | flops 2097152 | bytes 12582912 | tf_op jit(solution)/shard_map/convert_element_type | solution.py:48
  285.7 0.0 reduce-scatter.2.cloned.1.call-update
  285.8 38.0 %reduce-scatter.2.cloned.1.call-done = bf16[1024,256]{1,0:T(8,128)(2,1)} async-done(((bf16[8192,256]{1,0:T(8,128)(2,1)}), bf16[1024,256]{1,0:T(8,128)(2,1)}) %reduce-scatter.2.cloned.1.call-update) | async-done | bytes 524304 | tf_op jit(solution)/shard_map/reduce_scatter | solution.py:47
  323.8 2.1 convert_element_type.19
  325.9 0.0 copy-done.1
  (1 shorter events, 0.0 us)
Async XLA Ops:
  6.5 76.1 %copy-start = (bf16[4,256,256]{2,1,0:T(8,128)(2,1)S(1)}, bf16[4,256,256]{2,1,0:T(8,128)(2,1)}, u32[]{:S(2)}) copy-start(bf16[4,256,256]{2,1,0:T(8,128)(2,1)} %param.9) | copy-start | bytes 1572868
  6.5 76.1 %all-gather.2.cloned.1.call-start = ((), (), s32[]{:S(2)}) async-start(), calls=%async_computation.1 | async-start | bytes 8912896 | tf_op jit(solution)/shard_map/all_gather | solution.py:18
  7.3 316.5 %reduce-scatter.2.cloned.1.call-start = ((), (), s32[]{:S(2)}) async-start(), calls=%async_computation.2 | async-start | bytes 4718592 | tf_op jit(solution)/shard_map/reduce_scatter | solution.py:47
  177.9 4.2 %copy-start.2 = (s32[192]{0:T(256)S(1)}, s32[192]{0:T(256)}, u32[]{:S(2)}) copy-start(s32[192]{0:T(256)} %param.12) | copy-start | bytes 2308
  177.9 4.2 %copy-start.3 = (s32[192]{0:T(256)S(1)}, s32[192]{0:T(256)}, u32[]{:S(2)}) copy-start(s32[192]{0:T(256)} %param.11) | copy-start | bytes 2308
  279.7 46.1 %copy-start.1 = (bf16[4,256,256]{2,1,0:T(8,128)(2,1)S(1)}, bf16[4,256,256]{2,1,0:T(8,128)(2,1)}, u32[]{:S(2)}) copy-start(bf16[4,256,256]{2,1,0:T(8,128)(2,1)} %param.9) | copy-start | bytes 1572868
Sparse Core Ops, SparseCore 0:
  9.5 73.1 all-gather.1
  285.9 37.8 reduce-scatter.1
where the time goes:
time: 335 us; the launch traced here: 333 us
  waiting for transfers between devices  112 us (33%)
  local copies, waits for them, and re-layouts  98.6 us (29%)
  other arithmetic  68.4 us (20%)
  matrix products  40.1 us (12%)
  between operations  13.4 us (4%)
    all_gather x1, waiting for transfers between devices, per_device(): lax.all_gather(grad_out, 'col', axis=0, tiled=True)  73.3 us
    scatter-add x3, other arithmetic, step(): return partial_value.at[col_part].add(term)  58.6 us
    reshape x1, local copies, waits for them, and re-layouts, per_device(): table = gathered.reshape(ncols * owned, blk, kinds, feat)  54.7 us
    reduce_scatter x1, waiting for transfers between devices, per_device(): lax.psum_scatter(partial_value.reshape(nrows * owned * blk, feat).astype(...  38 us
    while x1, local copies, waits for them, and re-layouts, per_device(): partial_value = lax.fori_loop(0, groups, step, partial_start)  23 us
    dot_general x3, matrix products, step(): jnp.einsum('kab,kaf->kbf', adj_part, picked, preferred_element_type=jnp.f...  22.7 us
    dot_general x1, matrix products, per_device(): jnp.dot(lax.all_gather(grad_out, 'col', axis=0, tiled=True), wcat, prefer...  17.5 us
    gather x3, local copies, waits for them, and re-layouts, step(): picked = table[slot_part, :, kind_part, :]  15.9 us
  transfers between devices with their start and end apart: 2, of which 2 were waited for; matrix products, arithmetic and copies ran while one was open for 1% of the time, Pallas kernels for 0%

commit v1 on v0

--- a/solution.py
+++ b/solution.py
@@ -3,6 +3,24 @@
 import jax.numpy as jnp
 from jax import lax
 from jax.sharding import PartitionSpec as P
+
+
+def collect(array, axis, dim):
+    ways, here, step = (lax.axis_size(axis), lax.axis_index(axis), array.shape[dim])
+    shape = [n * ways if d == dim else n for d, n in enumerate(array.shape)]
+    full = lax.dynamic_update_slice_in_dim(
+        jnp.zeros(shape, array.dtype), array, here * step, axis=dim
+    )
+    going_up = going_down = array
+    for far in range(1, ways // 2 + 1):
+        going_up = lax.ppermute(going_up, axis, [(d, (d + 1) % ways) for d in range(ways)])
+        full = lax.dynamic_update_slice_in_dim(full, going_up, (here - far) % ways * step, axis=dim)
+        if 2 * far < ways:
+            going_down = lax.ppermute(going_down, axis, [(d, (d - 1) % ways) for d in range(ways)])
+            full = lax.dynamic_update_slice_in_dim(
+                full, going_down, (here + far) % ways * step, axis=dim
+            )
+    return full
 
 
 def per_device(grad_out, rel_weight, adjacency, block_row, block_col, type_count):
@@ -15,9 +33,7 @@
     slots_total = adjacency.shape[0]
     wcat = jnp.transpose(rel_weight, (2, 0, 1)).reshape(feat, kinds * feat)
     gathered = jnp.dot(
-        lax.all_gather(grad_out, "col", axis=0, tiled=True),
-        wcat,
-        preferred_element_type=jnp.float32,
+        collect(grad_out, "col", 0), wcat, preferred_element_type=jnp.float32
     ).astype(jnp.bfloat16)
     table = gathered.reshape(ncols * owned, blk, kinds, feat)
     ends = jnp.cumsum(type_count)

time: 335 us -> 373 us (1.11)
  starting transfers between devices: 0.04 us -> 37.5 us
  local copies, waits for them, and re-layouts: 98.6 us -> 122 us
  waiting for transfers between devices: 112 us -> 89.3 us
    all_gather x1 -> x0, waiting for transfers between devices: 73.3 us -> none  [per_device(): lax.all_gather(grad_out, 'col', axis=0, tiled=True)]
    ppermute x0 -> x15, waiting for transfers between devices: none -> 54.2 us  [the longest x8 53.8 us: collect(): lax.ppermute(going_up, axis, [(d, (d + 1) % ways) for d in range(ways)])]
    ppermute x0 -> x15, starting transfers between devices: none -> 37.5 us  [the longest x7 35.9 us: collect(): lax.ppermute(going_down, axis, [(d, (d - 1) % ways) for d in range(ways)])]
    dynamic_update_slice x0 -> x16, local copies, waits for them, and re-layouts: none -> 19.7 us  [the longest x8 9.83 us: collect(): lax.dynamic_update_slice_in_dim(full, going_up, (here - far) % ways * ste...]
  transfers between devices with their start and end apart: 2 -> 16, of which waited for: 2 -> 9; matrix products, arithmetic and copies ran while one was open for 1% -> 7% of each run, Pallas kernels for 0% -> 0%
where the time goes in v1:
time: 373 us; the launch traced here: 371 us
  local copies, waits for them, and re-layouts  122 us (33%)
  waiting for transfers between devices  89.3 us (24%)
  other arithmetic  68.4 us (18%)
  matrix products  40.2 us (11%)
  starting transfers between devices  37.5 us (10%)
  between operations  13.7 us (4%)
    scatter-add x3, other arithmetic, step(): return partial_value.at[col_part].add(term)  58.4 us
    reshape x1, local copies, waits for them, and re-layouts, per_device(): table = gathered.reshape(ncols * owned, blk, kinds, feat)  54.7 us
    ppermute x8, waiting for transfers between devices, collect(): lax.ppermute(going_up, axis, [(d, (d + 1) % ways) for d in range(ways)])  53.8 us
    ppermute x7, starting transfers between devices, collect(): lax.ppermute(going_down, axis, [(d, (d - 1) % ways) for d in range(ways)])  35.9 us
    reduce_scatter x1, waiting for transfers between devices, per_device(): lax.psum_scatter(partial_value.reshape(nrows * owned * blk, feat).astype(...  35.1 us
    while x1, local copies, waits for them, and re-layouts, per_device(): partial_value = lax.fori_loop(0, groups, step, partial_start)  23 us
    dot_general x3, matrix products, step(): jnp.einsum('kab,kaf->kbf', adj_part, picked, preferred_element_type=jnp.f...  22.7 us
    dot_general x1, matrix products, per_device(): jnp.dot(collect(grad_out, 'col', 0), wcat, preferred_element_type=jnp.flo...  17.5 us
  transfers between devices with their start and end apart: 16, of which 9 were waited for; matrix products, arithmetic and copies ran while one was open for 7% of the time, Pallas kernels for 0%

profile of v1, /device:TPU:0, one launch (start us, length us, event | category | flops | bytes accessed | tf_op | source)
XLA Modules:
  0.0 370.9 jit_solution(16858302423752766840)
XLA Ops:
  6.5 1.6 collective-permute-start
  8.1 3.8 %collective-permute-start.1 = (bf16[1024,256]{1,0:T(8,128)(2,1)}, bf16[1024,256]{1,0:T(8,128)(2,1)S(1)}, u32[]{:S(2)}, u32[]{:S(2)}) collective-permute-start(bf16[1024,256]{1,0:T(8,128)(2,1)} %param.8), channel_id=1, source_target_pairs={{0,15},{1,0},{2,1},{3,2},{4,3},{5,4},{6,5},{7,6},{8,7},{9,8},{10,9... | collective-permute-start | bytes 1572872 | tf_op jit(solution)/shard_map/ppermute | solution.py:19
  11.9 12.1 %collective-permute-done = bf16[1024,256]{1,0:T(8,128)(2,1)S(1)} collective-permute-done((bf16[1024,256]{1,0:T(8,128)(2,1)}, bf16[1024,256]{1,0:T(8,128)(2,1)S(1)}, u32[]{:S(2)}, u32[]{:S(2)}) %collective-permute-start) | collective-permute-done | bytes 524320 | tf_op jit(solution)/shard_map/ppermute | solution.py:16
  24.0 5.3 %collective-permute-start.3 = (bf16[1024,256]{1,0:T(8,128)(2,1)S(1)}, bf16[1024,256]{1,0:T(8,128)(2,1)S(1)}, u32[]{:S(2)}, u32[]{:S(2)}) collective-permute-start(bf16[1024,256]{1,0:T(8,128)(2,1)S(1)} %collective-permute-done.1), channel_id=1, source_target_pairs={{0,15},{1,0},{2,1},{3,2},{4,3},{5,4},{6,5},{7,6},{8,7},{9,8},{10,9... | collective-permute-start | bytes 1572872 | tf_op jit(solution)/shard_map/ppermute | solution.py:19
  29.4 11.1 %collective-permute-done.2 = bf16[1024,256]{1,0:T(8,128)(2,1)S(1)} collective-permute-done((bf16[1024,256]{1,0:T(8,128)(2,1)S(1)}, bf16[1024,256]{1,0:T(8,128)(2,1)S(1)}, u32[]{:S(2)}, u32[]{:S(2)}) %collective-permute-start.2) | collective-permute-done | bytes 524320 | tf_op jit(solution)/shard_map/ppermute | solution.py:16
  40.5 5.3 %collective-permute-start.5 = (bf16[1024,256]{1,0:T(8,128)(2,1)S(1)}, bf16[1024,256]{1,0:T(8,128)(2,1)S(1)}, u32[]{:S(2)}, u32[]{:S(2)}) collective-permute-start(bf16[1024,256]{1,0:T(8,128)(2,1)S(1)} %collective-permute-done.3), channel_id=1, source_target_pairs={{0,15},{1,0},{2,1},{3,2},{4,3},{5,4},{6,5},{7,6},{8,7},{9,8},{10,9... | collective-permute-start | bytes 1572872 | tf_op jit(solution)/shard_map/ppermute | solution.py:19
  45.8 10.2 %collective-permute-done.4 = bf16[1024,256]{1,0:T(8,128)(2,1)S(1)} collective-permute-done((bf16[1024,256]{1,0:T(8,128)(2,1)S(1)}, bf16[1024,256]{1,0:T(8,128)(2,1)S(1)}, u32[]{:S(2)}, u32[]{:S(2)}) %collective-permute-start.4) | collective-permute-done | bytes 524320 | tf_op jit(solution)/shard_map/ppermute | solution.py:16
  56.0 5.3 %collective-permute-start.7 = (bf16[1024,256]{1,0:T(8,128)(2,1)S(1)}, bf16[1024,256]{1,0:T(8,128)(2,1)}, u32[]{:S(2)}, u32[]{:S(2)}) collective-permute-start(bf16[1024,256]{1,0:T(8,128)(2,1)S(1)} %collective-permute-done.5), channel_id=1, source_target_pairs={{0,15},{1,0},{2,1},{3,2},{4,3},{5,4},{6,5},{7,6},{8,7},{9,8},{10,9... | collective-permute-start | bytes 1572872 | tf_op jit(solution)/shard_map/ppermute | solution.py:19
  61.3 9.5 %collective-permute-done.6 = bf16[1024,256]{1,0:T(8,128)(2,1)} collective-permute-done((bf16[1024,256]{1,0:T(8,128)(2,1)S(1)}, bf16[1024,256]{1,0:T(8,128)(2,1)}, u32[]{:S(2)}, u32[]{:S(2)}) %collective-permute-start.6) | collective-permute-done | bytes 524320 | tf_op jit(solution)/shard_map/ppermute | solution.py:16
  70.8 0.8 reduce-window.4
  71.7 5.4 %collective-permute-start.9 = (bf16[1024,256]{1,0:T(8,128)(2,1)}, bf16[1024,256]{1,0:T(8,128)(2,1)}, u32[]{:S(2)}, u32[]{:S(2)}) collective-permute-start(bf16[1024,256]{1,0:T(8,128)(2,1)} %collective-permute-done.7), channel_id=1, source_target_pairs={{0,15},{1,0},{2,1},{3,2},{4,3},{5,4},{6,5},{7,6},{8,7},{9,8},{10,9... | collective-permute-start | bytes 1572872 | tf_op jit(solution)/shard_map/ppermute | solution.py:19
  77.1 3.7 broadcast_in_dim.57
  80.8 0.8 constant_dynamic-update-slice_fusion.15
  82.3 2.7 collective-permute-done.8
  85.9 0.9 constant_dynamic-update-slice_fusion.14
  86.8 1.9 constant_dynamic-update-slice_fusion.13
  88.7 1.9 constant_dynamic-update-slice_fusion.12
  90.5 5.3 %collective-permute-start.11 = (bf16[1024,256]{1,0:T(8,128)(2,1)}, bf16[1024,256]{1,0:T(8,128)(2,1)S(1)}, u32[]{:S(2)}, u32[]{:S(2)}) collective-permute-start(bf16[1024,256]{1,0:T(8,128)(2,1)} %collective-permute-done.9), channel_id=1, source_target_pairs={{0,15},{1,0},{2,1},{3,2},{4,3},{5,4},{6,5},{7,6},{8,7},{9,8},{10,9... | collective-permute-start | bytes 1572872 | tf_op jit(solution)/shard_map/ppermute | solution.py:19
  95.8 0.8 constant_dynamic-update-slice_fusion.11
  96.7 1.5 collective-permute-done.10
  99.8 1.9 constant_dynamic-update-slice_fusion.8
  101.7 1.9 constant_dynamic-update-slice_fusion.7
  103.6 5.4 %collective-permute-start.13 = (bf16[1024,256]{1,0:T(8,128)(2,1)S(1)}, bf16[1024,256]{1,0:T(8,128)(2,1)S(1)}, u32[]{:S(2)}, u32[]{:S(2)}) collective-permute-start(bf16[1024,256]{1,0:T(8,128)(2,1)S(1)} %collective-permute-done.11), channel_id=1, source_target_pairs={{0,15},{1,0},{2,1},{3,2},{4,3},{5,4},{6,5},{7,6},{8,7},{9,8},{10,9... | collective-permute-start | bytes 1572872 | tf_op jit(solution)/shard_map/ppermute | solution.py:19
  108.9 1.9 constant_dynamic-update-slice_fusion.6
  110.8 1.9 constant_dynamic-update-slice_fusion.5
  112.7 0.8 constant_dynamic-update-slice_fusion.4
  113.5 0.9 constant_dynamic-update-slice_fusion.3
  114.4 0.9 constant_dynamic-update-slice_fusion.2
  115.6 0.8 constant_dynamic-update-slice_fusion.1
  116.5 6.8 %collective-permute-done.14 = bf16[1024,256]{1,0:T(8,128)(2,1)S(1)} collective-permute-done((bf16[1024,256]{1,0:T(8,128)(2,1)S(1)}, bf16[1024,256]{1,0:T(8,128)(2,1)S(1)}, u32[]{:S(2)}, u32[]{:S(2)}) %collective-permute-start.14) | collective-permute-done | bytes 524320 | tf_op jit(solution)/shard_map/ppermute | solution.py:16
  123.3 0.8 constant_dynamic-update-slice_fusion
  124.1 17.5 %convolution_convert_fusion = bf16[16384,1024]{1,0:T(8,128)(2,1)} fusion(bf16[16384,256]{1,0:T(8,128)(2,1)} %constant_dynamic-update-slice_fusion, bf16[256,1024]{0,1:T(8,128)(2,1)S(1)} %bitcast.12), kind=kOutput, calls=%fused_computation.13 | convolution fusion | flops 8606711808 | bytes 42467328 | tf_op jit(solution)/shard_map/dot_general | solution.py:35
  141.6 54.7 %reshape.19 = bf16[128,128,4,256]{3,2,1,0:T(4,128)(2,1)} reshape(bf16[16384,1024]{1,0:T(8,128)(2,1)} %convolution_convert_fusion) | data formatting | bytes 67108864 | tf_op jit(solution)/shard_map/reshape | solution.py:38
  196.3 23.0 %copy.12 = bf16[128,128,4,256]{3,1,2,0:T(8,128)(2,1)} copy(bf16[128,128,4,256]{3,2,1,0:T(4,128)(2,1)} %reshape.19) | data formatting | bytes 67108864 | tf_op jit(solution)/shard_map/while | solution.py:62
  219.4 4.2 %broadcast_in_dim.56 = f32[64,128,256]{2,1,0:T(8,128)} broadcast(f32[]{:T(128)} %constant.143.clone.1), dimensions={} | broadcast | bytes 8388612 | tf_op jit(solution)/shard_map/broadcast_in_dim | solution.py:48
  223.6 97.2 %while.13 = (s32[]{:T(128)}, f32[64,128,256]{2,1,0:T(8,128)}, s32[192]{0:T(256)S(1)}, pred[192]{0:T(512)(128)(4,1)S(1)}, bf16[192,128,128]{2,1,0:T(8,128)(2,1)},...) while((s32[]{:T(128)}, f32[64,128,256]{2,1,0:T(8,128)}, ...), condition=%wide.region_4.5_spmd, body=%wide.region_2.4_spmd.sunk | while | flops 541066112 | bytes 48236912 | solution.py:62
  223.7 5.1 %gather_fusion = bf16[64,128,256]{2,1,0:T(8,128)(2,1)} fusion(bf16[128,128,4,256]{3,1,2,0:T(8,128)(2,1)} %get-tuple-element.271, s32[64]{0:T(128)S(1)} %get-tuple-element.239), kind=kCustom, calls=%fused_computation.clone.1 | custom fusion | bytes 8389120 | tf_op jit(solution)/shard_map/while/body/eval_jaxpr/gather | solution.py:57
  228.8 7.6 %broadcast_select_fusion.2 = f32[64,128,256]{2,1,0:T(8,128)} fusion(pred[64]{0:T(512)(128)(4,1)S(1)} %dynamic_slice.45, bf16[64,128,256]{2,1,0:T(8,128)(2,1)} %gather_fusion, bf16[192,128,128]{2,1,0:T(8,128)(2,1)} %get-tuple-element.268, s32[]{:T(128)S(6)} %select_n.203), kind=kOutput, calls=%fused_computation.2.clone.1 | convolution fusion | flops 538968064 | bytes 14680132 | tf_op jit(solution)/shard_map/while/body/eval_jaxpr/kab,kaf->kbf/dot_general | solution.py:58
  236.4 19.5 %scatter_fusion = f32[64,128,256]{2,1,0:T(8,128)} fusion(f32[64,128,256]{2,1,0:T(8,128)} %get-tuple-element.253, s32[64]{0:T(128)S(1)} %get-tuple-element.238, f32[64,128,256]{2,1,0:T(8,128)} %broadcast_select_fusion.2), kind=kCustom, calls=%fused_computation.1.clone.1 | custom fusion | flops 2097152 | bytes 25166080 | tf_op jit(solution)/shard_map/while/body/eval_jaxpr/scatter-add | solution.py:60
  255.9 5.4 %gather_fusion = bf16[64,128,256]{2,1,0:T(8,128)(2,1)} fusion(bf16[128,128,4,256]{3,1,2,0:T(8,128)(2,1)} %get-tuple-element.271, s32[64]{0:T(128)S(1)} %get-tuple-element.239), kind=kCustom, calls=%fused_computation.clone.1 | custom fusion | bytes 8389120 | tf_op jit(solution)/shard_map/while/body/eval_jaxpr/gather | solution.py:57
  261.4 7.6 %broadcast_select_fusion.2 = f32[64,128,256]{2,1,0:T(8,128)} fusion(pred[64]{0:T(512)(128)(4,1)S(1)} %dynamic_slice.45, bf16[64,128,256]{2,1,0:T(8,128)(2,1)} %gather_fusion, bf16[192,128,128]{2,1,0:T(8,128)(2,1)} %get-tuple-element.268, s32[]{:T(128)S(6)} %select_n.203), kind=kOutput, calls=%fused_computation.2.clone.1 | convolution fusion | flops 538968064 | bytes 14680132 | tf_op jit(solution)/shard_map/while/body/eval_jaxpr/kab,kaf->kbf/dot_general | solution.py:58
  269.0 19.6 %scatter_fusion = f32[64,128,256]{2,1,0:T(8,128)} fusion(f32[64,128,256]{2,1,0:T(8,128)} %get-tuple-element.253, s32[64]{0:T(128)S(1)} %get-tuple-element.238, f32[64,128,256]{2,1,0:T(8,128)} %broadcast_select_fusion.2), kind=kCustom, calls=%fused_computation.1.clone.1 | custom fusion | flops 2097152 | bytes 25166080 | tf_op jit(solution)/shard_map/while/body/eval_jaxpr/scatter-add | solution.py:60
  288.6 5.1 %gather_fusion = bf16[64,128,256]{2,1,0:T(8,128)(2,1)} fusion(bf16[128,128,4,256]{3,1,2,0:T(8,128)(2,1)} %get-tuple-element.271, s32[64]{0:T(128)S(1)} %get-tuple-element.239), kind=kCustom, calls=%fused_computation.clone.1 | custom fusion | bytes 8389120 | tf_op jit(solution)/shard_map/while/body/eval_jaxpr/gather | solution.py:57
  293.9 7.6 %broadcast_select_fusion.2 = f32[64,128,256]{2,1,0:T(8,128)} fusion(pred[64]{0:T(512)(128)(4,1)S(1)} %dynamic_slice.45, bf16[64,128,256]{2,1,0:T(8,128)(2,1)} %gather_fusion, bf16[192,128,128]{2,1,0:T(8,128)(2,1)} %get-tuple-element.268, s32[]{:T(128)S(6)} %select_n.203), kind=kOutput, calls=%fused_computation.2.clone.1 | convolution fusion | flops 538968064 | bytes 14680132 | tf_op jit(solution)/shard_map/while/body/eval_jaxpr/kab,kaf->kbf/dot_general | solution.py:58
  301.4 19.4 %scatter_fusion = f32[64,128,256]{2,1,0:T(8,128)} fusion(f32[64,128,256]{2,1,0:T(8,128)} %get-tuple-element.253, s32[64]{0:T(128)S(1)} %get-tuple-element.238, f32[64,128,256]{2,1,0:T(8,128)} %broadcast_select_fusion.2), kind=kCustom, calls=%fused_computation.1.clone.1 | custom fusion | flops 2097152 | bytes 25166080 | tf_op jit(solution)/shard_map/while/body/eval_jaxpr/scatter-add | solution.py:60
  320.8 6.0 %convert_element_type.17 = bf16[64,128,256]{2,1,0:T(8,128)(2,1)} convert(f32[64,128,256]{2,1,0:T(8,128)} %get-tuple-element.144) | non-fusion elementwise | flops 2097152 | bytes 12582912 | tf_op jit(solution)/shard_map/convert_element_type | solution.py:64
  326.8 35.1 %reduce-scatter.2.cloned.1.call-done = bf16[1024,256]{1,0:T(8,128)(2,1)} async-done(((bf16[8192,256]{1,0:T(8,128)(2,1)}), bf16[1024,256]{1,0:T(8,128)(2,1)}) %reduce-scatter.2.cloned.1.call-update) | async-done | bytes 524304 | tf_op jit(solution)/shard_map/reduce_scatter | solution.py:63
  362.0 2.1 convert_element_type.19
  (43 shorter events, 4.0 us)
Async XLA Ops:
  6.5 117.6 %copy-start = (bf16[4,256,256]{2,1,0:T(8,128)(2,1)S(1)}, bf16[4,256,256]{2,1,0:T(8,128)(2,1)}, u32[]{:S(2)}) copy-start(bf16[4,256,256]{2,1,0:T(8,128)(2,1)} %param.9) | copy-start | bytes 1572868
  6.5 74.3 %copy-start.2 = (bf16[1024,256]{1,0:T(8,128)(2,1)S(1)}, bf16[1024,256]{1,0:T(8,128)(2,1)}, u32[]{:S(2)}) copy-start(bf16[1024,256]{1,0:T(8,128)(2,1)} %param.8) | copy-start | bytes 1572868
  6.5 355.4 %reduce-scatter.2.cloned.1.call-start = ((), (), s32[]{:S(2)}) async-start(), calls=%async_computation.1 | async-start | bytes 4718592 | tf_op jit(solution)/shard_map/reduce_scatter | solution.py:63
  6.5 17.5 %collective-permute-start = (bf16[1024,256]{1,0:T(8,128)(2,1)}, bf16[1024,256]{1,0:T(8,128)(2,1)S(1)}, u32[]{:S(2)}, u32[]{:S(2)}) collective-permute-start(bf16[1024,256]{1,0:T(8,128)(2,1)} %param.8), channel_id=1, source_target_pairs={{0,1},{1,2},{2,3},{3,4},{4,5},{5,6},{6,7},{7,8},{8,9},{9,10},{10,1... | collective-permute-start | bytes 1572872 | tf_op jit(solution)/shard_map/ppermute | solution.py:16
  8.1 15.9 %collective-permute-start.1 = (bf16[1024,256]{1,0:T(8,128)(2,1)}, bf16[1024,256]{1,0:T(8,128)(2,1)S(1)}, u32[]{:S(2)}, u32[]{:S(2)}) collective-permute-start(bf16[1024,256]{1,0:T(8,128)(2,1)} %param.8), channel_id=1, source_target_pairs={{0,15},{1,0},{2,1},{3,2},{4,3},{5,4},{6,5},{7,6},{8,7},{9,8},{10,9... | collective-permute-start | bytes 1572872 | tf_op jit(solution)/shard_map/ppermute | solution.py:19
  24.0 16.4 %collective-permute-start.2 = (bf16[1024,256]{1,0:T(8,128)(2,1)S(1)}, bf16[1024,256]{1,0:T(8,128)(2,1)S(1)}, u32[]{:S(2)}, u32[]{:S(2)}) collective-permute-start(bf16[1024,256]{1,0:T(8,128)(2,1)S(1)} %collective-permute-done), channel_id=1, source_target_pairs={{0,1},{1,2},{2,3},{3,4},{4,5},{5,6},{6,7},{7,8},{8,9},{9,10},{10,1... | collective-permute-start | bytes 1572872 | tf_op jit(solution)/shard_map/ppermute | solution.py:16
  24.0 16.4 %copy-start.3 = (bf16[1024,256]{1,0:T(8,128)(2,1)}, bf16[1024,256]{1,0:T(8,128)(2,1)S(1)}, u32[]{:S(2)}) copy-start(bf16[1024,256]{1,0:T(8,128)(2,1)S(1)} %collective-permute-done.1) | copy-start | bytes 1572868
  24.0 16.4 %collective-permute-start.3 = (bf16[1024,256]{1,0:T(8,128)(2,1)S(1)}, bf16[1024,256]{1,0:T(8,128)(2,1)S(1)}, u32[]{:S(2)}, u32[]{:S(2)}) collective-permute-start(bf16[1024,256]{1,0:T(8,128)(2,1)S(1)} %collective-permute-done.1), channel_id=1, source_target_pairs={{0,15},{1,0},{2,1},{3,2},{4,3},{5,4},{6,5},{7,6},{8,7},{9,8},{10,9... | collective-permute-start | bytes 1572872 | tf_op jit(solution)/shard_map/ppermute | solution.py:19
  40.4 30.4 %copy-start.4 = (bf16[1024,256]{1,0:T(8,128)(2,1)}, bf16[1024,256]{1,0:T(8,128)(2,1)S(1)}, u32[]{:S(2)}) copy-start(bf16[1024,256]{1,0:T(8,128)(2,1)S(1)} %collective-permute-done.2) | copy-start | bytes 1572868
  40.4 15.6 %collective-permute-start.4 = (bf16[1024,256]{1,0:T(8,128)(2,1)S(1)}, bf16[1024,256]{1,0:T(8,128)(2,1)S(1)}, u32[]{:S(2)}, u32[]{:S(2)}) collective-permute-start(bf16[1024,256]{1,0:T(8,128)(2,1)S(1)} %collective-permute-done.2), channel_id=1, source_target_pairs={{0,1},{1,2},{2,3},{3,4},{4,5},{5,6},{6,7},{7,8},{8,9},{9,10},{10,1... | collective-permute-start | bytes 1572872 | tf_op jit(solution)/shard_map/ppermute | solution.py:16
  40.5 15.5 %collective-permute-start.5 = (bf16[1024,256]{1,0:T(8,128)(2,1)S(1)}, bf16[1024,256]{1,0:T(8,128)(2,1)S(1)}, u32[]{:S(2)}, u32[]{:S(2)}) collective-permute-start(bf16[1024,256]{1,0:T(8,128)(2,1)S(1)} %collective-permute-done.3), channel_id=1, source_target_pairs={{0,15},{1,0},{2,1},{3,2},{4,3},{5,4},{6,5},{7,6},{8,7},{9,8},{10,9... | collective-permute-start | bytes 1572872 | tf_op jit(solution)/shard_map/ppermute | solution.py:19
  56.0 14.8 %collective-permute-start.6 = (bf16[1024,256]{1,0:T(8,128)(2,1)S(1)}, bf16[1024,256]{1,0:T(8,128)(2,1)}, u32[]{:S(2)}, u32[]{:S(2)}) collective-permute-start(bf16[1024,256]{1,0:T(8,128)(2,1)S(1)} %collective-permute-done.4), channel_id=1, source_target_pairs={{0,1},{1,2},{2,3},{3,4},{4,5},{5,6},{6,7},{7,8},{8,9},{9,10},{10,1... | collective-permute-start | bytes 1572872 | tf_op jit(solution)/shard_map/ppermute | solution.py:16
  56.0 15.7 %collective-permute-start.7 = (bf16[1024,256]{1,0:T(8,128)(2,1)S(1)}, bf16[1024,256]{1,0:T(8,128)(2,1)}, u32[]{:S(2)}, u32[]{:S(2)}) collective-permute-start(bf16[1024,256]{1,0:T(8,128)(2,1)S(1)} %collective-permute-done.5), channel_id=1, source_target_pairs={{0,15},{1,0},{2,1},{3,2},{4,3},{5,4},{6,5},{7,6},{8,7},{9,8},{10,9... | collective-permute-start | bytes 1572872 | tf_op jit(solution)/shard_map/ppermute | solution.py:19
  70.8 14.2 %collective-permute-start.8 = (bf16[1024,256]{1,0:T(8,128)(2,1)}, bf16[1024,256]{1,0:T(8,128)(2,1)}, u32[]{:S(2)}, u32[]{:S(2)}) collective-permute-start(bf16[1024,256]{1,0:T(8,128)(2,1)} %collective-permute-done.6), channel_id=1, source_target_pairs={{0,1},{1,2},{2,3},{3,4},{4,5},{5,6},{6,7},{7,8},{8,9},{9,10},{10,1... | collective-permute-start | bytes 1572872 | tf_op jit(solution)/shard_map/ppermute | solution.py:16
  71.7 18.8 %collective-permute-start.9 = (bf16[1024,256]{1,0:T(8,128)(2,1)}, bf16[1024,256]{1,0:T(8,128)(2,1)}, u32[]{:S(2)}, u32[]{:S(2)}) collective-permute-start(bf16[1024,256]{1,0:T(8,128)(2,1)} %collective-permute-done.7), channel_id=1, source_target_pairs={{0,15},{1,0},{2,1},{3,2},{4,3},{5,4},{6,5},{7,6},{8,7},{9,8},{10,9... | collective-permute-start | bytes 1572872 | tf_op jit(solution)/shard_map/ppermute | solution.py:19
  85.0 13.2 %collective-permute-start.10 = (bf16[1024,256]{1,0:T(8,128)(2,1)}, bf16[1024,256]{1,0:T(8,128)(2,1)S(1)}, u32[]{:S(2)}, u32[]{:S(2)}) collective-permute-start(bf16[1024,256]{1,0:T(8,128)(2,1)} %collective-permute-done.8), channel_id=1, source_target_pairs={{0,1},{1,2},{2,3},{3,4},{4,5},{5,6},{6,7},{7,8},{8,9},{9,10},{10,1... | collective-permute-start | bytes 1572872 | tf_op jit(solution)/shard_map/ppermute | solution.py:16
  90.5 13.0 %collective-permute-start.11 = (bf16[1024,256]{1,0:T(8,128)(2,1)}, bf16[1024,256]{1,0:T(8,128)(2,1)S(1)}, u32[]{:S(2)}, u32[]{:S(2)}) collective-permute-start(bf16[1024,256]{1,0:T(8,128)(2,1)} %collective-permute-done.9), channel_id=1, source_target_pairs={{0,15},{1,0},{2,1},{3,2},{4,3},{5,4},{6,5},{7,6},{8,7},{9,8},{10,9... | collective-permute-start | bytes 1572872 | tf_op jit(solution)/shard_map/ppermute | solution.py:19
  98.1 12.7 %collective-permute-start.12 = (bf16[1024,256]{1,0:T(8,128)(2,1)S(1)}, bf16[1024,256]{1,0:T(8,128)(2,1)S(1)}, u32[]{:S(2)}, u32[]{:S(2)}) collective-permute-start(bf16[1024,256]{1,0:T(8,128)(2,1)S(1)} %collective-permute-done.10), channel_id=1, source_target_pairs={{0,1},{1,2},{2,3},{3,4},{4,5},{5,6},{6,7},{7,8},{8,9},{9,10},{10,1... | collective-permute-start | bytes 1572872 | tf_op jit(solution)/shard_map/ppermute | solution.py:16
  103.6 12.1 %collective-permute-start.13 = (bf16[1024,256]{1,0:T(8,128)(2,1)S(1)}, bf16[1024,256]{1,0:T(8,128)(2,1)S(1)}, u32[]{:S(2)}, u32[]{:S(2)}) collective-permute-start(bf16[1024,256]{1,0:T(8,128)(2,1)S(1)} %collective-permute-done.11), channel_id=1, source_target_pairs={{0,15},{1,0},{2,1},{3,2},{4,3},{5,4},{6,5},{7,6},{8,7},{9,8},{10,9... | collective-permute-start | bytes 1572872 | tf_op jit(solution)/shard_map/ppermute | solution.py:19
  110.8 12.5 %collective-permute-start.14 = (bf16[1024,256]{1,0:T(8,128)(2,1)S(1)}, bf16[1024,256]{1,0:T(8,128)(2,1)S(1)}, u32[]{:S(2)}, u32[]{:S(2)}) collective-permute-start(bf16[1024,256]{1,0:T(8,128)(2,1)S(1)} %collective-permute-done.12), channel_id=1, source_target_pairs={{0,1},{1,2},{2,3},{3,4},{4,5},{5,6},{6,7},{7,8},{8,9},{9,10},{10,1... | collective-permute-start | bytes 1572872 | tf_op jit(solution)/shard_map/ppermute | solution.py:16
  219.3 4.2 %copy-start.5 = (s32[192]{0:T(256)S(1)}, s32[192]{0:T(256)}, u32[]{:S(2)}) copy-start(s32[192]{0:T(256)} %param.12) | copy-start | bytes 2308
  219.3 4.2 %copy-start.6 = (s32[192]{0:T(256)S(1)}, s32[192]{0:T(256)}, u32[]{:S(2)}) copy-start(s32[192]{0:T(256)} %param.11) | copy-start | bytes 2308
  320.8 43.3 %copy-start.1 = (bf16[4,256,256]{2,1,0:T(8,128)(2,1)S(1)}, bf16[4,256,256]{2,1,0:T(8,128)(2,1)}, u32[]{:S(2)}) copy-start(bf16[4,256,256]{2,1,0:T(8,128)(2,1)} %param.9) | copy-start | bytes 1572868
Sparse Core Ops, SparseCore 0:
  327.0 34.9 reduce-scatter.1
